TPU v7x, 32 devices: a whole 2x2x4 slice. The times are simulated.
32 devices in a mesh: rep: 8 (over y, x, core), tp: 4 (over z).
Axes of the slice: x: 2, y: 2, z: 4, core: 2. Of those that a mesh axis runs over, the one named last changes fastest.
Arguments:
- hidden: bfloat16 [512, 8192], P('rep'), may hold values from -6 to 6
- norm_gain: bfloat16 [8192], replicated, may hold values from 0.5 to 1.5
- query_weight_matrix: bfloat16 [8192, 4096], P(None, 'tp'), may hold values from -0.0625 to 0.0625
- key_value_weight: bfloat16 [2, 8192, 1024], P(None, None, 'tp'), may hold values from -0.0625 to 0.0625
- output_weight_matrix: bfloat16 [4096, 8192], P('tp'), may hold values from -0.375 to 0.375
- input_down_factors: bfloat16 [3, 8192, 64], P(None, ('rep', 'tp')), may hold values from -0.0625 to 0.0625
- query_up_factor: bfloat16 [64, 4096], P(None, ('rep', 'tp')), may hold values from -0.75 to 0.75
- key_value_up_factors: bfloat16 [2, 64, 1024], P(None, None, ('rep', 'tp')), may hold values from -0.75 to 0.75
- output_down_factor: bfloat16 [4096, 64], P(('rep', 'tp')), may hold values from -0.375 to 0.375
- output_up_factor: bfloat16 [64, 8192], P(None, ('rep', 'tp')), may hold values from -0.75 to 0.75
- cache_keys: bfloat16 [512, 8, 128, 128], P('rep', 'tp'), may hold values from -360 to 360
- cache_values: bfloat16 [512, 8, 128, 128], P('rep', 'tp'), may hold values from -6 to 6
- lengths: int32 [512], P('rep'), may hold values from 1 to 127
Outputs:
- attn_out: bfloat16 [512, 8192], P('rep', 'tp')
All inputs are finite; a program needn't handle non-finite values.
Results may differ from a plain program's by a relative error of at most 0.03.
Values may be sent and summed in bfloat16 or wider, within the bound.
A program may use at most 128 MiB of HBM per device.

v0:
```python
import math
import jax
import jax.numpy as jnp
from jax import lax
from jax.sharding import PartitionSpec as P

epsilon = 1e-06
rope_base = 1000000.0
adapter_scale = 0.5


def rope_angles(lengths, head_dim):
    half_dim = head_dim // 2
    frequency = rope_base ** (-(jnp.arange(half_dim, dtype=jnp.float32) * 2.0) / head_dim)
    return lengths.astype(jnp.float32)[:, None] * frequency[None, :]


def rotate(vectors, angles):
    half_dim = vectors.shape[-1] // 2
    cosine = jnp.cos(angles)[:, None, :]
    sine_part = jnp.sin(angles)[:, None, :]
    low_half = vectors[..., :half_dim]
    high_half = vectors[..., half_dim:]
    return jnp.concatenate(
        [low_half * cosine - high_half * sine_part, high_half * cosine + low_half * sine_part],
        axis=-1,
    )


def adapted(normed, frozen_matrix, inner_part, up_factor):
    base_part = jnp.dot(normed, frozen_matrix, preferred_element_type=jnp.float32)
    return base_part + adapter_scale * jnp.dot(
        inner_part, up_factor, preferred_element_type=jnp.float32
    )


def attend(query, new_key, new_value, keys, values, lengths):
    score_scale = 1.0 / math.sqrt(keys.shape[-1])
    scores = (
        jnp.einsum(
            "bkgd,bkld->bkgl", query, keys.astype(jnp.float32), precision=lax.Precision.HIGHEST
        )
        * score_scale
    )
    own_score = jnp.sum(query * new_key.astype(jnp.float32)[:, :, None, :], axis=-1) * score_scale
    live_mask = (
        jnp.arange(keys.shape[2], dtype=jnp.int32)[None, None, None, :]
        < lengths[:, None, None, None]
    )
    row_max = jnp.maximum(jnp.max(jnp.where(live_mask, scores, -1e30), axis=-1), own_score)
    weights = jnp.where(live_mask, jnp.exp(scores - row_max[..., None]), 0.0)
    own_weight = jnp.exp(own_score - row_max)
    denom_sum = jnp.sum(weights, axis=-1) + own_weight
    probs = (weights / denom_sum[..., None]).astype(jnp.bfloat16)
    own_prob = (own_weight / denom_sum).astype(jnp.bfloat16)
    context = jnp.einsum("bkgl,bkld->bkgd", probs, values, preferred_element_type=jnp.float32)
    context = (
        context
        + own_prob.astype(jnp.float32)[..., None] * new_value.astype(jnp.float32)[:, :, None, :]
    )
    return context.astype(jnp.bfloat16)


def regroup(factor, tp_count, group):
    count, rank_dim, wide = factor.shape
    return factor.reshape(count, rank_dim, tp_count, group, wide // (tp_count * group))


def settle(factor):
    count, rank_dim, tp_count, group, piece = factor.shape
    return jnp.swapaxes(factor, 2, 3).reshape(count, rank_dim, group * tp_count * piece)


def local(
    hidden,
    norm_gain,
    query_weight_matrix,
    key_value_weight,
    output_weight_matrix,
    input_down_factors,
    query_up_factor,
    key_value_up_factors,
    output_down_factor,
    output_up_factor,
    cache_keys,
    cache_values,
    lengths,
):
    states = hidden.astype(jnp.float32)
    square = jnp.mean(states * states, axis=-1, keepdims=True)
    normed = (states * lax.rsqrt(square + epsilon) * norm_gain.astype(jnp.float32)).astype(
        jnp.bfloat16
    )
    seq_count = hidden.shape[0]
    block_rows = input_down_factors.shape[1]
    rep_count = lax.axis_size("rep")
    tp_count = lax.axis_size("tp")
    tp_index = lax.axis_index("tp")
    own_features = lax.dynamic_slice_in_dim(
        normed.reshape(seq_count, rep_count, tp_count, block_rows), tp_index, 1, 2
    )
    own_features = own_features.reshape(seq_count, rep_count * block_rows)
    partial_inner = jnp.einsum(
        "bd,jdr->jbr",
        own_features,
        lax.all_gather(input_down_factors, "rep", axis=1, tiled=True),
        preferred_element_type=jnp.float32,
    )
    inner = lax.psum(partial_inner.astype(jnp.bfloat16), "tp")
    query_up_rows = query_up_factor[None]
    out_down_rows = jnp.swapaxes(output_down_factor, 0, 1)[None]
    out_up_rows = output_up_factor[None]
    per_rep = (
        lax.all_gather(query_up_rows, "rep", axis=2, tiled=True),
        lax.all_gather(key_value_up_factors, "rep", axis=2, tiled=True),
        lax.all_gather(out_down_rows, "rep", axis=2, tiled=True),
        lax.all_gather(out_up_rows, "rep", axis=2, tiled=True),
    )
    group = rep_count // tp_count
    arrived = (
        lax.all_to_all(
            regroup(per_rep[0], tp_count, group), "tp", split_axis=2, concat_axis=2, tiled=True
        ),
        lax.all_to_all(
            regroup(per_rep[1], tp_count, group), "tp", split_axis=2, concat_axis=2, tiled=True
        ),
        lax.all_to_all(
            regroup(per_rep[2], tp_count, group), "tp", split_axis=2, concat_axis=2, tiled=True
        ),
        lax.all_to_all(
            regroup(per_rep[3], tp_count, group), "tp", split_axis=2, concat_axis=2, tiled=True
        ),
    )
    query_up_local = settle(arrived[0])
    key_value_up_local = settle(arrived[1])
    out_down_local = settle(arrived[2])
    out_up_local = settle(arrived[3])
    kv_local = cache_keys.shape[1]
    head_dim = cache_keys.shape[3]
    angles = rope_angles(lengths, head_dim)
    query = adapted(normed, query_weight_matrix, inner[0], query_up_local[0]).reshape(
        seq_count, -1, head_dim
    )
    query = rotate(query, angles).reshape(seq_count, kv_local, -1, head_dim)
    new_key = adapted(normed, key_value_weight[0], inner[1], key_value_up_local[0]).reshape(
        seq_count, kv_local, head_dim
    )
    new_key = rotate(new_key, angles).astype(jnp.bfloat16)
    new_value = (
        adapted(normed, key_value_weight[1], inner[2], key_value_up_local[1])
        .reshape(seq_count, kv_local, head_dim)
        .astype(jnp.bfloat16)
    )
    context = attend(query, new_key, new_value, cache_keys, cache_values, lengths).reshape(
        seq_count, -1
    )
    partial_middle = jnp.einsum(
        "bh,rh->br", context, out_down_local[0], preferred_element_type=jnp.float32
    )
    middle = lax.psum(partial_middle, "tp").astype(jnp.bfloat16)
    partial_value = jnp.dot(context, output_weight_matrix, preferred_element_type=jnp.float32)
    summed = lax.psum_scatter(
        partial_value.astype(jnp.bfloat16), "tp", scatter_dimension=1, tiled=True
    ).astype(jnp.float32)
    summed = summed + adapter_scale * jnp.dot(
        middle, out_up_local[0], preferred_element_type=jnp.float32
    )
    return summed.astype(jnp.bfloat16)


def solution(mesh):
    return jax.shard_map(
        local,
        mesh=mesh,
        in_specs=(
            P("rep", None),
            P(),
            P(None, "tp"),
            P(None, None, "tp"),
            P("tp", None),
            P(None, ("rep", "tp"), None),
            P(None, ("rep", "tp")),
            P(None, None, ("rep", "tp")),
            P(("rep", "tp"), None),
            P(None, ("rep", "tp")),
            P("rep", "tp", None, None),
            P("rep", "tp", None, None),
            P("rep"),
        ),
        out_specs=P("rep", "tp"),
        check_vma=False,
    )
```

profile of v0, /device:TPU:0, one launch (start us, length us, event | category | flops | bytes accessed | tf_op | source)
XLA Modules:
  0.0 177.4 jit_solution(7634904349694602952)
XLA Ops:
  6.5 10.9 %all_gather.17 = bf16[2,64,256]{1,2,0:T(8,128)(2,1)S(1)} all-gather(bf16[2,64,32]{1,2,0:T(8,128)(2,1)} %param.20), channel_id=1, replica_groups=mesh['rep'=8,'tp'=4] {'rep'}, dimensions={2}, use_global_device_ids=true | all-gather | bytes 73728 | tf_op jit(solution)/shard_map/all_gather | solution.py:115
  18.2 4.9 %all-to-all-start.1 = ((bf16[4,2,4096]{2,1,0:T(2,128)(2,1)}), bf16[4,2,4096]{2,1,0:T(2,128)(2,1)S(1)}, u32[]{:S(2)}, u32[]{:S(2)}) async-start(bf16[4,2,4096]{2,1,0:T(2,128)(2,1)} %reshape.203), calls=%async_computation.1 | async-start | bytes 131072 | tf_op jit(solution)/shard_map/all_to_all | solution.py:124
  23.8 1.5 fusion.8
  25.4 1.5 fusion.10
  26.9 0.8 reshape.182
  27.7 3.0 %fusion.2 = f32[64,256]{1,0:T(8,128)S(1)} fusion(bf16[64,8192]{1,0:T(8,128)(2,1)S(1)} %fusion.10, bf16[2,8192,256]{2,1,0:T(8,128)(2,1)} %param.16), kind=kOutput, calls=%fused_computation.3 | convolution fusion | flops 268435456 | bytes 5308416 | tf_op jit(solution)/shard_map/dot_general | solution.py:31
  30.7 3.0 %fusion = f32[64,256]{1,0:T(8,128)S(1)} fusion(bf16[64,8192]{1,0:T(8,128)(2,1)S(1)} %fusion.10, bf16[2,8192,256]{2,1,0:T(8,128)(2,1)} %param.16), kind=kOutput, calls=%fused_computation.1 | convolution fusion | flops 268435456 | bytes 5308416 | tf_op jit(solution)/shard_map/dot_general | solution.py:31
  33.8 1.5 dynamic-slice_reduce_fusion
  35.5 12.6 %all_gather.15 = bf16[3,2048,64]{1,2,0:T(8,128)(2,1)S(1)} all-gather(bf16[3,256,64]{1,2,0:T(8,128)(2,1)S(1)} %copy-done), channel_id=1, replica_groups=mesh['rep'=8,'tp'=4] {'rep'}, dimensions={1}, use_global_device_ids=true | all-gather | bytes 884736 | tf_op jit(solution)/shard_map/all_gather | solution.py:106
  48.8 8.3 %all-gather = bf16[64,1024]{1,0:T(8,128)(2,1)S(1)} all-gather(bf16[64,128]{1,0:T(8,128)(2,1)S(1)} %copy-done.2), channel_id=2, replica_groups=mesh['rep'=8,'tp'=4] {'rep'}, dimensions={1}, use_global_device_ids=true | all-gather | bytes 147456 | tf_op jit(solution)/shard_map/all_gather | solution.py:114
  57.9 19.8 %psum.14 = bf16[3,64,64]{2,1,0:T(8,128)(2,1)S(1)} all-reduce(bf16[3,64,64]{2,1,0:T(8,128)(2,1)S(1)} %fusion.17), channel_id=1, replica_groups=mesh['rep'=8,'tp'=4] {'tp'}, use_global_device_ids=true, to_apply=%region_1.0 | all-reduce | flops 12288 | bytes 49152 | tf_op jit(solution)/shard_map/psum | solution.py:109
  77.7 3.3 %all-to-all-start = ((bf16[1,64,4,2,128]{4,3,1,0,2:T(2,128)(2,1)}), bf16[1,64,4,2,128]{4,3,1,0,2:T(2,128)(2,1)S(1)}, u32[]{:S(2)}, u32[]{:S(2)}) async-start(bf16[1,64,4,2,128]{4,3,1,0,2:T(2,128)(2,1)} %copy.50), calls=%async_computation | async-start | bytes 262144 | tf_op jit(solution)/shard_map/all_to_all | solution.py:121
  82.2 4.7 %all-to-all-done = bf16[1,64,4,2,128]{4,3,1,0,2:T(2,128)(2,1)S(1)} async-done(((bf16[1,64,4,2,128]{4,3,1,0,2:T(2,128)(2,1)}), bf16[1,64,4,2,128]{4,3,1,0,2:T(2,128)(2,1)S(1)}, u32[]{:S(2)}, u32[]{:S(2)}) %all-to-all-start) | async-done | bytes 131104 | tf_op jit(solution)/shard_map/all_to_all | solution.py:121
  87.4 8.8 %fusion.11 = f32[8,8,8,128]{3,1,2,0:T(8,128)S(1)} fusion(f32[64,1024]{1,0:T(8,128)S(1)} %convolution_multiply_fusion.2, bf16[64,8192]{1,0:T(8,128)(2,1)S(1)} %fusion.10, bf16[8192,1024]{1,0:T(8,128)(2,1)} %param.15), kind=kOutput, calls=%fused_computation.19 | convolution fusion | flops 1073807360 | bytes 18350080 | tf_op jit(solution)/shard_map/dot_general | solution.py:31
  97.1 8.5 %select_reduce_fusion = (f32[64,2,4]{2,1,0:T(2,128)S(1)}, f32[64,2,4,128]{3,2,1,0:T(4,128)S(1)}) fusion(pred[64,128]{1,0:T(8,128)(4,1)S(1)} %iota_compare_fusion, f32[64,2,4,128]{3,2,1,0:T(4,128)S(1)} %bitcast.58, bf16[64,2,128,128]{3,2,1,0:T(8,128)(2,1)} %param.23), kind=kOutput, calls=%fused_computation.34 | convolution fusion | flops 100859392 | bytes 4728832 | tf_op jit(solution)/shard_map/bkgd,bkld->bkgl/dot_general | solution.py:40
  106.6 3.5 %fusion.12 = bf16[64,2,4,128]{3,2,1,0:T(4,128)(2,1)S(1)} fusion(bf16[64,2,128,128]{3,2,1,0:T(8,128)(2,1)} %param.24, f32[64,2,4,128]{3,2,1,0:T(4,128)S(1)} %get-tuple-element.16, f32[64,2,128]{2,1,0:T(2,128)S(1)} %reshape.192, f32[64,2,4]{2,1,0:T(2,128)S(1)} %copy.59, f32[64,2,4]{2,1,0:T(2,128)S(1)} %copy.58, f32[64,2,4]{2,1,0:T(2,128)S(1)} %copy.56, ...), kind=kOutput, calls=%fused_computation.20 | convolution fusion | flops 17235968 | bytes 4667392 | tf_op jit(solution)/shard_map/bkgl,bkld->bkgd/dot_general | solution.py:56
  110.2 9.8 %convolution_convert_fusion = bf16[64,8192]{1,0:T(8,128)(2,1)} fusion(bf16[64,1024]{1,0:T(8,128)(2,1)S(1)} %reshape.189, bf16[1024,8192]{1,0:T(8,128)(2,1)} %param.17), kind=kOutput, calls=%fused_computation | convolution fusion | flops 1074266112 | bytes 17956864 | tf_op jit(solution)/shard_map/dot_general | solution.py:161
  120.0 8.2 %all-gather.1 = bf16[64,1024]{1,0:T(8,128)(2,1)S(1)} all-gather(bf16[64,128]{1,0:T(8,128)(2,1)S(1)} %bitcast.66), channel_id=3, replica_groups=mesh['rep'=8,'tp'=4] {'rep'}, dimensions={1}, use_global_device_ids=true | all-gather | bytes 147456 | tf_op jit(solution)/shard_map/all_gather | solution.py:116
  129.0 3.3 %all-to-all-start.2 = ((bf16[1,64,4,2,128]{4,3,1,0,2:T(2,128)(2,1)}), bf16[1,64,4,2,128]{4,3,1,0,2:T(2,128)(2,1)S(1)}, u32[]{:S(2)}, u32[]{:S(2)}) async-start(bf16[1,64,4,2,128]{4,3,1,0,2:T(2,128)(2,1)} %copy.61), calls=%async_computation.3 | async-start | bytes 262144 | tf_op jit(solution)/shard_map/all_to_all | solution.py:127
  132.3 9.8 %all-gather.2 = bf16[64,2048]{1,0:T(8,128)(2,1)S(1)} all-gather(bf16[64,256]{1,0:T(8,128)(2,1)S(1)} %copy-done.1), channel_id=4, replica_groups=mesh['rep'=8,'tp'=4] {'rep'}, dimensions={1}, use_global_device_ids=true | all-gather | bytes 294912 | tf_op jit(solution)/shard_map/all_gather | solution.py:117
  142.2 0.9 copy.63
  143.1 5.0 %all-to-all-start.3 = ((bf16[1,64,4,2,256]{4,3,1,0,2:T(2,128)(2,1)}), bf16[1,64,4,2,256]{4,3,1,0,2:T(2,128)(2,1)S(1)}, u32[]{:S(2)}, u32[]{:S(2)}) async-start(bf16[1,64,4,2,256]{4,3,1,0,2:T(2,128)(2,1)} %copy.63), calls=%async_computation.4 | async-start | bytes 524288 | tf_op jit(solution)/shard_map/all_to_all | solution.py:130
  148.6 19.5 %psum.15 = bf16[64,64]{1,0:T(8,128)(2,1)S(1)} all-reduce(f32[64,64]{1,0:T(8,128)S(1)} %fusion.29), channel_id=1, replica_groups=mesh['rep'=8,'tp'=4] {'tp'}, use_global_device_ids=true, to_apply=%region_6.7 | all-reduce | flops 4096 | bytes 24576 | tf_op jit(solution)/shard_map/psum | solution.py:160
  168.7 1.9 %fusion.7 = bf16[64,2048]{1,0:T(8,128)(2,1)} fusion(bf16[64,2048]{1,0:T(8,128)(2,1)S(1)} %squeeze_reshape.11, bf16[64,2048]{1,0:T(8,128)(2,1)} %reduce-scatter.2.cloned.1.call-done, bf16[64,64]{1,0:T(8,128)(2,1)S(1)} %psum.15), kind=kOutput, calls=%fused_computation.11 | convolution fusion | flops 17301504 | bytes 794624 | tf_op jit(solution)/shard_map/dot_general | solution.py:165
  (64 shorter events, 8.6 us)
Async XLA Ops:
  18.2 59.5 %all-to-all-start.1 = ((bf16[4,2,4096]{2,1,0:T(2,128)(2,1)}), bf16[4,2,4096]{2,1,0:T(2,128)(2,1)S(1)}, u32[]{:S(2)}, u32[]{:S(2)}) async-start(bf16[4,2,4096]{2,1,0:T(2,128)(2,1)} %reshape.203), calls=%async_computation.1 | async-start | bytes 131072 | tf_op jit(solution)/shard_map/all_to_all | solution.py:124
  30.7 4.7 %copy-start = (bf16[3,256,64]{1,2,0:T(8,128)(2,1)S(1)}, bf16[3,256,64]{1,2,0:T(8,128)(2,1)}, u32[]{:S(2)}) copy-start(bf16[3,256,64]{1,2,0:T(8,128)(2,1)} %param.18) | copy-start | bytes 294916
  30.7 17.3 %copy-start.4 = (s32[64]{0:T(128)S(1)}, s32[64]{0:T(128)}, u32[]{:S(2)}) copy-start(s32[64]{0:T(128)} %param.25) | copy-start | bytes 772
  30.7 18.0 %copy-start.2 = (bf16[64,128]{1,0:T(8,128)(2,1)S(1)}, bf16[64,128]{1,0:T(8,128)(2,1)}, u32[]{:S(2)}) copy-start(bf16[64,128]{1,0:T(8,128)(2,1)} %param.19) | copy-start | bytes 49156
  77.7 9.2 %all-to-all-start = ((bf16[1,64,4,2,128]{4,3,1,0,2:T(2,128)(2,1)}), bf16[1,64,4,2,128]{4,3,1,0,2:T(2,128)(2,1)S(1)}, u32[]{:S(2)}, u32[]{:S(2)}) async-start(bf16[1,64,4,2,128]{4,3,1,0,2:T(2,128)(2,1)} %copy.50), calls=%async_computation | async-start | bytes 262144 | tf_op jit(solution)/shard_map/all_to_all | solution.py:121
  81.1 87.6 %reduce-scatter.2.cloned.1.call-start = ((), (), s32[]{:S(2)}) async-start(), calls=%async_computation.5 | async-start | bytes 1310720 | tf_op jit(solution)/shard_map/reduce_scatter | solution.py:162
  110.2 9.8 %copy-start.3 = (bf16[128,64]{0,1:T(8,128)(2,1)S(1)}, bf16[128,64]{0,1:T(8,128)(2,1)}, u32[]{:S(2)}) copy-start(bf16[128,64]{0,1:T(8,128)(2,1)} %param.21) | copy-start | bytes 49156
  110.2 22.1 %copy-start.1 = (bf16[64,256]{1,0:T(8,128)(2,1)S(1)}, bf16[64,256]{1,0:T(8,128)(2,1)}, u32[]{:S(2)}) copy-start(bf16[64,256]{1,0:T(8,128)(2,1)} %param.22) | copy-start | bytes 98308
  129.0 14.2 %all-to-all-start.2 = ((bf16[1,64,4,2,128]{4,3,1,0,2:T(2,128)(2,1)}), bf16[1,64,4,2,128]{4,3,1,0,2:T(2,128)(2,1)S(1)}, u32[]{:S(2)}, u32[]{:S(2)}) async-start(bf16[1,64,4,2,128]{4,3,1,0,2:T(2,128)(2,1)} %copy.61), calls=%async_computation.3 | async-start | bytes 262144 | tf_op jit(solution)/shard_map/all_to_all | solution.py:127
  143.1 25.0 %all-to-all-start.3 = ((bf16[1,64,4,2,256]{4,3,1,0,2:T(2,128)(2,1)}), bf16[1,64,4,2,256]{4,3,1,0,2:T(2,128)(2,1)S(1)}, u32[]{:S(2)}, u32[]{:S(2)}) async-start(bf16[1,64,4,2,256]{4,3,1,0,2:T(2,128)(2,1)} %copy.63), calls=%async_computation.4 | async-start | bytes 524288 | tf_op jit(solution)/shard_map/all_to_all | solution.py:130
Sparse Core Ops, SparseCore 0:
  120.1 27.4 reduce-scatter.1
where the time goes:
time: 178 us; the launch traced here: 177 us
  blocking collectives  89 us (50%)
  matrix products  39.5 us (22%)
  starting transfers between devices  16.8 us (9%)
  between operations  13.8 us (8%)
  local copies, waits for them, and re-layouts  7.97 us (4%)
  other arithmetic  5.58 us (3%)
  waiting for transfers between devices  4.78 us (3%)
    psum x1, blocking collectives, local(): inner = lax.psum(partial_inner.astype(jnp.bfloat16), 'tp')  19.8 us
    psum x1, blocking collectives, local(): middle = lax.psum(partial_middle, 'tp').astype(jnp.bfloat16)  19.5 us
    dot_general x3, matrix products, adapted(): jnp.dot(normed, frozen_matrix, preferred_element_type=jnp.float32)  14.8 us
    all_gather x1, blocking collectives, local(): lax.all_gather(input_down_factors, 'rep', axis=1, tiled=True)  12.6 us
    all_gather x1, blocking collectives, local(): lax.all_gather(key_value_up_factors, 'rep', axis=2, tiled=True)  10.9 us
    dot_general x1, matrix products, local(): jnp.dot(context, output_weight_matrix, preferred_element_type=jnp.float32)  9.79 us
    all_gather x1, blocking collectives, local(): lax.all_gather(out_up_rows, 'rep', axis=2, tiled=True)  9.75 us
    dot_general x1, matrix products, attend(): jnp.einsum('bkgd,bkld->bkgl', query, keys.astype(jnp.float32), precision=...  8.5 us
  transfers between devices with their start and end apart: 5, of which 1 were waited for; matrix products, arithmetic and copies ran while one was open for 10% of the time, Pallas kernels for 0%

commit v1 on v0

--- a/solution.py
+++ b/solution.py
@@ -7,6 +7,10 @@
 epsilon = 1e-06
 rope_base = 1000000.0
 adapter_scale = 0.5
+
+
+def render_slots(body, axis_tag):
+    return jnp.concatenate(lax.all_gather(body, axis_name=axis_tag), 2)
 
 
 def rope_angles(lengths, head_dim):
@@ -114,7 +118,7 @@
         lax.all_gather(query_up_rows, "rep", axis=2, tiled=True),
         lax.all_gather(key_value_up_factors, "rep", axis=2, tiled=True),
         lax.all_gather(out_down_rows, "rep", axis=2, tiled=True),
-        lax.all_gather(out_up_rows, "rep", axis=2, tiled=True),
+        render_slots(out_up_rows, "rep"),
     )
     group = rep_count // tp_count
     arrived = (

time: 178 us -> 178 us (level)
  transfers between devices with their start and end apart: 5 -> 5, of which waited for: 1 -> 2; matrix products, arithmetic and copies ran while one was open for 10% -> 9% of each run, Pallas kernels for 0% -> 0%
where the time goes in v1:
time: 178 us; the launch traced here: 177 us
  blocking collectives  89.4 us (50%)
  matrix products  39.5 us (22%)
  starting transfers between devices  16.2 us (9%)
  between operations  13.8 us (8%)
  local copies, waits for them, and re-layouts  6.78 us (4%)
  other arithmetic  5.58 us (3%)
  waiting for transfers between devices  5.41 us (3%)
    psum x1, blocking collectives, local(): inner = lax.psum(partial_inner.astype(jnp.bfloat16), 'tp')  19.8 us
    psum x1, blocking collectives, local(): middle = lax.psum(partial_middle, 'tp').astype(jnp.bfloat16)  19.5 us
    dot_general x3, matrix products, adapted(): jnp.dot(normed, frozen_matrix, preferred_element_type=jnp.float32)  14.8 us
    all_gather x1, blocking collectives, local(): lax.all_gather(input_down_factors, 'rep', axis=1, tiled=True)  12.6 us
    all_gather x1, blocking collectives, local(): lax.all_gather(key_value_up_factors, 'rep', axis=2, tiled=True)  10.9 us
    all_gather x1, blocking collectives, render_slots(): return jnp.concatenate(lax.all_gather(body, axis_name=axis_tag), 2)  10.2 us
    dot_general x1, matrix products, local(): jnp.dot(context, output_weight_matrix, preferred_element_type=jnp.float32)  9.79 us
    dot_general x1, matrix products, attend(): jnp.einsum('bkgd,bkld->bkgl', query, keys.astype(jnp.float32), precision=...  8.5 us
  transfers between devices with their start and end apart: 5, of which 2 were waited for; matrix products, arithmetic and copies ran while one was open for 9% of the time, Pallas kernels for 0%

profile of v1, /device:TPU:0, one launch (start us, length us, event | category | flops | bytes accessed | tf_op | source)
XLA Modules:
  0.0 176.7 jit_solution(2396097959677634321)
XLA Ops:
  6.5 10.9 %all_gather.17 = bf16[2,64,256]{1,2,0:T(8,128)(2,1)S(1)} all-gather(bf16[2,64,32]{1,2,0:T(8,128)(2,1)} %param.20), channel_id=1, replica_groups=mesh['rep'=8,'tp'=4] {'rep'}, dimensions={2}, use_global_device_ids=true | all-gather | bytes 73728 | tf_op jit(solution)/shard_map/all_gather | solution.py:119
  17.4 0.8 reshape.202
  18.2 4.9 %all-to-all-start.1 = ((bf16[4,2,4096]{2,1,0:T(2,128)(2,1)}), bf16[4,2,4096]{2,1,0:T(2,128)(2,1)S(1)}, u32[]{:S(2)}, u32[]{:S(2)}) async-start(bf16[4,2,4096]{2,1,0:T(2,128)(2,1)} %reshape.202), calls=%async_computation.1 | async-start | bytes 131072 | tf_op jit(solution)/shard_map/all_to_all | solution.py:128
  23.8 1.5 fusion.8
  25.4 1.5 fusion.10
  26.9 0.8 reshape.182
  27.7 3.0 %fusion.2 = f32[64,256]{1,0:T(8,128)S(1)} fusion(bf16[64,8192]{1,0:T(8,128)(2,1)S(1)} %fusion.10, bf16[2,8192,256]{2,1,0:T(8,128)(2,1)} %param.16), kind=kOutput, calls=%fused_computation.3 | convolution fusion | flops 268435456 | bytes 5308416 | tf_op jit(solution)/shard_map/dot_general | solution.py:35
  30.7 3.0 %fusion = f32[64,256]{1,0:T(8,128)S(1)} fusion(bf16[64,8192]{1,0:T(8,128)(2,1)S(1)} %fusion.10, bf16[2,8192,256]{2,1,0:T(8,128)(2,1)} %param.16), kind=kOutput, calls=%fused_computation.1 | convolution fusion | flops 268435456 | bytes 5308416 | tf_op jit(solution)/shard_map/dot_general | solution.py:35
  33.8 1.5 dynamic-slice_reduce_fusion
  35.5 12.6 %all_gather.15 = bf16[3,2048,64]{1,2,0:T(8,128)(2,1)S(1)} all-gather(bf16[3,256,64]{1,2,0:T(8,128)(2,1)S(1)} %copy-done), channel_id=1, replica_groups=mesh['rep'=8,'tp'=4] {'rep'}, dimensions={1}, use_global_device_ids=true | all-gather | bytes 884736 | tf_op jit(solution)/shard_map/all_gather | solution.py:110
  48.8 8.3 %all-gather = bf16[64,1024]{1,0:T(8,128)(2,1)S(1)} all-gather(bf16[64,128]{1,0:T(8,128)(2,1)S(1)} %copy-done.2), channel_id=2, replica_groups=mesh['rep'=8,'tp'=4] {'rep'}, dimensions={1}, use_global_device_ids=true | all-gather | bytes 147456 | tf_op jit(solution)/shard_map/all_gather | solution.py:118
  57.9 19.8 %psum.14 = bf16[3,64,64]{2,1,0:T(8,128)(2,1)S(1)} all-reduce(bf16[3,64,64]{2,1,0:T(8,128)(2,1)S(1)} %fusion.17), channel_id=1, replica_groups=mesh['rep'=8,'tp'=4] {'tp'}, use_global_device_ids=true, to_apply=%region_1.0 | all-reduce | flops 12288 | bytes 49152 | tf_op jit(solution)/shard_map/psum | solution.py:113
  77.7 3.3 %all-to-all-start = ((bf16[1,64,4,2,128]{4,3,1,0,2:T(2,128)(2,1)}), bf16[1,64,4,2,128]{4,3,1,0,2:T(2,128)(2,1)S(1)}, u32[]{:S(2)}, u32[]{:S(2)}) async-start(bf16[1,64,4,2,128]{4,3,1,0,2:T(2,128)(2,1)} %copy.55), calls=%async_computation | async-start | bytes 262144 | tf_op jit(solution)/shard_map/all_to_all | solution.py:125
  82.2 4.7 %all-to-all-done = bf16[1,64,4,2,128]{4,3,1,0,2:T(2,128)(2,1)S(1)} async-done(((bf16[1,64,4,2,128]{4,3,1,0,2:T(2,128)(2,1)}), bf16[1,64,4,2,128]{4,3,1,0,2:T(2,128)(2,1)S(1)}, u32[]{:S(2)}, u32[]{:S(2)}) %all-to-all-start) | async-done | bytes 131104 | tf_op jit(solution)/shard_map/all_to_all | solution.py:125
  87.4 8.8 %fusion.11 = f32[8,8,8,128]{3,1,2,0:T(8,128)S(1)} fusion(f32[64,1024]{1,0:T(8,128)S(1)} %convolution_multiply_fusion.2, bf16[64,8192]{1,0:T(8,128)(2,1)S(1)} %fusion.10, bf16[8192,1024]{1,0:T(8,128)(2,1)} %param.15), kind=kOutput, calls=%fused_computation.19 | convolution fusion | flops 1073807360 | bytes 18350080 | tf_op jit(solution)/shard_map/dot_general | solution.py:35
  97.1 8.5 %select_reduce_fusion = (f32[64,2,4]{2,1,0:T(2,128)S(1)}, f32[64,2,4,128]{3,2,1,0:T(4,128)S(1)}) fusion(pred[64,128]{1,0:T(8,128)(4,1)S(1)} %iota_compare_fusion, f32[64,2,4,128]{3,2,1,0:T(4,128)S(1)} %bitcast.65, bf16[64,2,128,128]{3,2,1,0:T(8,128)(2,1)} %param.23), kind=kOutput, calls=%fused_computation.34 | convolution fusion | flops 100859392 | bytes 4728832 | tf_op jit(solution)/shard_map/bkgd,bkld->bkgl/dot_general | solution.py:44
  106.6 3.5 %fusion.12 = bf16[64,2,4,128]{3,2,1,0:T(4,128)(2,1)S(1)} fusion(bf16[64,2,128,128]{3,2,1,0:T(8,128)(2,1)} %param.24, f32[64,2,4,128]{3,2,1,0:T(4,128)S(1)} %get-tuple-element.16, f32[64,2,128]{2,1,0:T(2,128)S(1)} %reshape.192, f32[64,2,4]{2,1,0:T(2,128)S(1)} %copy.64, f32[64,2,4]{2,1,0:T(2,128)S(1)} %copy.63, f32[64,2,4]{2,1,0:T(2,128)S(1)} %copy.61, ...), kind=kOutput, calls=%fused_computation.20 | convolution fusion | flops 17235968 | bytes 4667392 | tf_op jit(solution)/shard_map/bkgl,bkld->bkgd/dot_general | solution.py:60
  110.2 9.8 %convolution_convert_fusion = bf16[64,8192]{1,0:T(8,128)(2,1)} fusion(bf16[64,1024]{1,0:T(8,128)(2,1)S(1)} %reshape.189, bf16[1024,8192]{1,0:T(8,128)(2,1)} %param.17), kind=kOutput, calls=%fused_computation | convolution fusion | flops 1074266112 | bytes 17956864 | tf_op jit(solution)/shard_map/dot_general | solution.py:165
  120.0 8.2 %all-gather.1 = bf16[64,1024]{1,0:T(8,128)(2,1)S(1)} all-gather(bf16[64,128]{1,0:T(8,128)(2,1)S(1)} %bitcast.73), channel_id=3, replica_groups=mesh['rep'=8,'tp'=4] {'rep'}, dimensions={1}, use_global_device_ids=true | all-gather | bytes 147456 | tf_op jit(solution)/shard_map/all_gather | solution.py:120
  129.0 3.3 %all-to-all-start.2 = ((bf16[1,64,4,2,128]{4,3,1,0,2:T(2,128)(2,1)}), bf16[1,64,4,2,128]{4,3,1,0,2:T(2,128)(2,1)S(1)}, u32[]{:S(2)}, u32[]{:S(2)}) async-start(bf16[1,64,4,2,128]{4,3,1,0,2:T(2,128)(2,1)} %copy.66), calls=%async_computation.3 | async-start | bytes 262144 | tf_op jit(solution)/shard_map/all_to_all | solution.py:131
  132.3 10.2 %all-gather.2 = bf16[512,256]{1,0:T(8,128)(2,1)} all-gather(bf16[64,256]{1,0:T(8,128)(2,1)S(1)} %copy-done.1), channel_id=4, replica_groups=mesh['rep'=8,'tp'=4] {'rep'}, dimensions={0}, use_global_device_ids=true | all-gather | bytes 294912 | tf_op jit(solution)/shard_map/all_gather | solution.py:13
  143.1 4.4 %all-to-all-start.3 = ((bf16[1,64,4,2,256]{4,1,3,0,2:T(8,128)(2,1)}), bf16[1,64,4,2,256]{4,1,3,0,2:T(8,128)(2,1)S(1)}, u32[]{:S(2)}, u32[]{:S(2)}) async-start(bf16[1,64,4,2,256]{4,1,3,0,2:T(8,128)(2,1)} %bitcast.19), calls=%async_computation.4 | async-start | bytes 524288 | tf_op jit(solution)/shard_map/all_to_all | solution.py:134
  148.0 19.5 %psum.15 = bf16[64,64]{1,0:T(8,128)(2,1)S(1)} all-reduce(f32[64,64]{1,0:T(8,128)S(1)} %fusion.29), channel_id=1, replica_groups=mesh['rep'=8,'tp'=4] {'tp'}, use_global_device_ids=true, to_apply=%region_6.7 | all-reduce | flops 4096 | bytes 24576 | tf_op jit(solution)/shard_map/psum | solution.py:164
  168.0 1.9 %fusion.7 = bf16[64,2048]{1,0:T(8,128)(2,1)} fusion(bf16[64,2048]{1,0:T(8,128)(2,1)S(1)} %squeeze_reshape.11, bf16[64,2048]{1,0:T(8,128)(2,1)} %reduce-scatter.2.cloned.1.call-done, bf16[64,64]{1,0:T(8,128)(2,1)S(1)} %psum.15), kind=kOutput, calls=%fused_computation.11 | convolution fusion | flops 17301504 | bytes 794624 | tf_op jit(solution)/shard_map/dot_general | solution.py:169
  (62 shorter events, 8.2 us)
Async XLA Ops:
  18.2 59.5 %all-to-all-start.1 = ((bf16[4,2,4096]{2,1,0:T(2,128)(2,1)}), bf16[4,2,4096]{2,1,0:T(2,128)(2,1)S(1)}, u32[]{:S(2)}, u32[]{:S(2)}) async-start(bf16[4,2,4096]{2,1,0:T(2,128)(2,1)} %reshape.202), calls=%async_computation.1 | async-start | bytes 131072 | tf_op jit(solution)/shard_map/all_to_all | solution.py:128
  30.7 4.7 %copy-start = (bf16[3,256,64]{1,2,0:T(8,128)(2,1)S(1)}, bf16[3,256,64]{1,2,0:T(8,128)(2,1)}, u32[]{:S(2)}) copy-start(bf16[3,256,64]{1,2,0:T(8,128)(2,1)} %param.18) | copy-start | bytes 294916
  30.7 17.3 %copy-start.4 = (s32[64]{0:T(128)S(1)}, s32[64]{0:T(128)}, u32[]{:S(2)}) copy-start(s32[64]{0:T(128)} %param.25) | copy-start | bytes 772
  30.7 18.0 %copy-start.2 = (bf16[64,128]{1,0:T(8,128)(2,1)S(1)}, bf16[64,128]{1,0:T(8,128)(2,1)}, u32[]{:S(2)}) copy-start(bf16[64,128]{1,0:T(8,128)(2,1)} %param.19) | copy-start | bytes 49156
  77.7 9.2 %all-to-all-start = ((bf16[1,64,4,2,128]{4,3,1,0,2:T(2,128)(2,1)}), bf16[1,64,4,2,128]{4,3,1,0,2:T(2,128)(2,1)S(1)}, u32[]{:S(2)}, u32[]{:S(2)}) async-start(bf16[1,64,4,2,128]{4,3,1,0,2:T(2,128)(2,1)} %copy.55), calls=%async_computation | async-start | bytes 262144 | tf_op jit(solution)/shard_map/all_to_all | solution.py:125
  81.1 86.9 %reduce-scatter.2.cloned.1.call-start = ((), (), s32[]{:S(2)}) async-start(), calls=%async_computation.5 | async-start | bytes 1310720 | tf_op jit(solution)/shard_map/reduce_scatter | solution.py:166
  110.2 9.8 %copy-start.3 = (bf16[128,64]{0,1:T(8,128)(2,1)S(1)}, bf16[128,64]{0,1:T(8,128)(2,1)}, u32[]{:S(2)}) copy-start(bf16[128,64]{0,1:T(8,128)(2,1)} %param.21) | copy-start | bytes 49156
  110.2 22.2 %copy-start.1 = (bf16[64,256]{1,0:T(8,128)(2,1)S(1)}, bf16[64,256]{1,0:T(8,128)(2,1)}, u32[]{:S(2)}) copy-start(bf16[64,256]{1,0:T(8,128)(2,1)} %param.22) | copy-start | bytes 98308
  129.0 14.2 %all-to-all-start.2 = ((bf16[1,64,4,2,128]{4,3,1,0,2:T(2,128)(2,1)}), bf16[1,64,4,2,128]{4,3,1,0,2:T(2,128)(2,1)S(1)}, u32[]{:S(2)}, u32[]{:S(2)}) async-start(bf16[1,64,4,2,128]{4,3,1,0,2:T(2,128)(2,1)} %copy.66), calls=%async_computation.3 | async-start | bytes 262144 | tf_op jit(solution)/shard_map/all_to_all | solution.py:131
  143.1 24.4 %all-to-all-start.3 = ((bf16[1,64,4,2,256]{4,1,3,0,2:T(8,128)(2,1)}), bf16[1,64,4,2,256]{4,1,3,0,2:T(8,128)(2,1)S(1)}, u32[]{:S(2)}, u32[]{:S(2)}) async-start(bf16[1,64,4,2,256]{4,1,3,0,2:T(8,128)(2,1)} %bitcast.19), calls=%async_computation.4 | async-start | bytes 524288 | tf_op jit(solution)/shard_map/all_to_all | solution.py:134
Sparse Core Ops, SparseCore 0:
  120.1 27.4 reduce-scatter.1
